TPU v7x, 256 devices: a whole 4x4x8 slice. The times are simulated.
256 devices in a mesh: tm: 64 (over z, y, core), freq: 4 (over x).
Axes of the slice: x: 4, y: 4, z: 8, core: 2. Of those that a mesh axis runs over, the one named last changes fastest.
Arguments:
- visibilities: bfloat16 [2, 64, 1024, 1024], P(None, 'freq', 'tm'), may hold values from -6 to 6
- projection: bfloat16 [128, 64, 2, 2, 64, 512], P('tm', 'freq'), may hold values from -0.1875 to 0.1875
- kl_weight: bfloat16 [128, 2, 64, 64], P('tm'), may hold values from -0.5 to 0.5
- azimuthal: int32 [128], replicated, may hold values from 0 to 1023, as said below
- live_mode_totals: int32 [128, 64, 2], P('tm', 'freq'), may hold values from 1 to 64, as said below
Outputs:
- kl_modes: float32 [128, 2, 64, 2, 64], P('tm', None, None, None, 'freq')
Inputs may be any that keep to these rules, and one draw needn't show every extreme that they name: `azimuthal`: the m values are distinct. `live_mode_totals`: slots from the count up to 64 are padding; the count 64 occurs in every draw.
All inputs are finite; a program needn't handle non-finite values.
Results may differ from a plain program's by a relative error of at most 0.012.
Values may be sent and summed in bfloat16 or wider, within the bound.
A program may use at most 192 MiB of HBM per device.

v0:
```python
import math

import jax
import jax.numpy as jnp
from jax import lax
from jax.sharding import PartitionSpec as P


def twiddle_tables(orders, time_index, time_total):
    phase_index = orders[:, None] * time_index[None, :] % time_total
    angles = phase_index.astype(jnp.float32) * (2.0 * math.pi / time_total)
    return jnp.stack([jnp.cos(angles), jnp.sin(angles)], axis=0)


def split_table(table):
    upper = table.astype(jnp.bfloat16)
    lower = (table - upper.astype(jnp.float32)).astype(jnp.bfloat16)
    return (upper, lower)


def time_transform(streams, tables, time_total):
    parts, chans, samples, columns = streams.shape
    orders_count = tables.shape[1]
    flat = jnp.transpose(streams, (2, 0, 1, 3)).reshape(samples, parts * chans * columns)
    cos_upper, cos_lower = split_table(tables[0])
    sin_upper, sin_lower = split_table(tables[1])
    stacked = jnp.concatenate([cos_upper, cos_lower, sin_upper, sin_lower], axis=0)
    product = jnp.dot(stacked, flat, preferred_element_type=jnp.float32)
    product = product.reshape(4, orders_count, parts, chans, columns)
    cos_part = product[0] + product[1]
    sin_part = product[2] + product[3]
    out_real = cos_part[:, 0] + sin_part[:, 1]
    out_imag = cos_part[:, 1] - sin_part[:, 0]
    return jnp.stack([out_real, out_imag], axis=2) * (1.0 / math.sqrt(time_total))


def kl_combine(kl_cols, regrouped):
    products = jnp.einsum(
        "srgc,scqpk->srqgpk", kl_cols, regrouped, preferred_element_type=jnp.float32
    )
    mixed_real = products[:, 0, 0] - products[:, 1, 1]
    mixed_imag = products[:, 0, 1] + products[:, 1, 0]
    return jnp.stack([mixed_real, mixed_imag], axis=1)


def shards(visibilities, projection, kl_weight, azimuthal, live_mode_totals):
    time_dev = visibilities.shape[2]
    time_total = time_dev * lax.axis_size("tm")
    channels_per_shard = visibilities.shape[1]
    mslot_total = projection.shape[0]
    polarization_total = projection.shape[2]
    baseline_pairs = projection.shape[5]
    mode_slots = projection.shape[4]
    time_index = jnp.arange(time_total, dtype=jnp.int32)
    tables = twiddle_tables(azimuthal, time_index, time_total)
    streams = lax.all_to_all(visibilities, "tm", split_axis=3, concat_axis=2, tiled=True)
    local_modes = time_transform(streams, tables, time_total).astype(jnp.bfloat16)
    mode_spectra = lax.all_to_all(local_modes, "tm", split_axis=0, concat_axis=3, tiled=True)
    mode_spectra = mode_spectra.reshape(
        mslot_total, channels_per_shard, 2, polarization_total, baseline_pairs
    )
    products = jnp.einsum(
        "scprkb,scqpb->scprqk", projection, mode_spectra, preferred_element_type=jnp.float32
    )
    proj_real = products[:, :, :, 0, 0] - products[:, :, :, 1, 1]
    proj_imag = products[:, :, :, 0, 1] + products[:, :, :, 1, 0]
    live_slots = (
        jnp.arange(mode_slots, dtype=jnp.int32)[None, None, None, :]
        < live_mode_totals[:, :, :, None]
    )
    stacked_modes = jnp.stack([proj_real, proj_imag], axis=2)
    projected = jnp.where(live_slots[:, :, None], stacked_modes, 0.0).astype(jnp.bfloat16)
    regrouped = lax.all_to_all(projected, "freq", split_axis=4, concat_axis=1, tiled=True)
    kl_modes = kl_combine(kl_weight, regrouped)
    return kl_modes


def solution(mesh):
    return jax.shard_map(
        shards,
        mesh=mesh,
        in_specs=(
            P(None, "freq", "tm", None),
            P("tm", "freq", None, None, None, None),
            P("tm", None, None, None),
            P(),
            P("tm", "freq", None),
        ),
        out_specs=P("tm", None, None, None, "freq"),
        check_vma=False,
    )
```

profile of v0, /device:TPU:1, one launch (start us, length us, event | category | flops | bytes accessed | tf_op | source)
XLA Modules:
  0.0 141.4 jit_solution(4933649290774078471)
XLA Ops:
  0.0 12.7 %copy.60 = bf16[2,16,16,1024]{2,1,0,3:T(8,128)(2,1)} copy(bf16[2,16,16,1024]{3,2,1,0:T(8,128)(2,1)} %param.5) | data formatting | bytes 2097152 | tf_op args[0]
  12.7 12.5 %reshape.137 = bf16[64,2,4096]{2,1,0:T(2,128)(2,1)} reshape(bf16[1024,2,16,16]{3,2,1,0:T(8,128)(2,1)} %bitcast.68) | data formatting | bytes 2097152
  25.2 13.2 %all-to-all-start = ((bf16[64,2,4096]{2,1,0:T(2,128)(2,1)}), bf16[64,2,4096]{2,1,0:T(2,128)(2,1)S(1)}, u32[]{:S(2)}, u32[]{:S(2)}) async-start(bf16[64,2,4096]{2,1,0:T(2,128)(2,1)} %reshape.137), calls=%async_computation | async-start | bytes 2097152 | tf_op jit(solution)/shard_map/all_to_all | solution.py:56
  38.3 2.5 %fusion.17 = (bf16[128,1024]{1,0:T(8,128)(2,1)S(1)}, bf16[128,1024]{1,0:T(8,128)(2,1)S(1)}, bf16[128,1024]{1,0:T(8,128)(2,1)S(1)}, bf16[128,1024]{1,0:T(8,128)(2,1)S(1)}) fusion(s32[128]{0:T(128)S(1)} %copy-done.2), kind=kLoop, calls=%fused_computation.27 | loop fusion | flops 2883584 | bytes 1049088 | tf_op jit(solution)/shard_map/convert_element_type | solution.py:16
  40.8 25.7 %all-to-all-done = bf16[64,2,4096]{2,1,0:T(2,128)(2,1)S(1)} async-done(((bf16[64,2,4096]{2,1,0:T(2,128)(2,1)}), bf16[64,2,4096]{2,1,0:T(2,128)(2,1)S(1)}, u32[]{:S(2)}, u32[]{:S(2)}) %all-to-all-start) | async-done | bytes 1048608 | tf_op jit(solution)/shard_map/all_to_all | solution.py:56
  66.5 7.5 %reshape.138 = bf16[1024,2,16,16]{3,2,1,0:T(8,128)(2,1)} reshape(bf16[64,2,4096]{2,1,0:T(2,128)(2,1)S(1)} %all-to-all-done) | data formatting | bytes 2097152
  74.0 12.0 %copy.62 = bf16[2,16,64,16,16]{3,2,4,1,0:T(8,128)(2,1)} copy(bf16[2,16,64,16,16]{3,1,0,4,2:T(8,128)(2,1)} %bitcast.69) | data formatting | bytes 2097152 | tf_op jit(solution)/shard_map/all_to_all | solution.py:56
  86.1 15.2 %all_to_all.40 = bf16[2,16,1024,16]{2,3,1,0:T(8,128)(2,1)S(1)} reshape(bf16[2,16,64,16,16]{3,2,4,1,0:T(8,128)(2,1)} %copy.62) | data formatting | bytes 2097152 | tf_op jit(solution)/shard_map/all_to_all | solution.py:56
  101.2 0.7 fusion
  102.1 0.9 copy.64
  103.0 1.8 %reshape.139 = bf16[64,2,512]{2,1,0:T(2,128)(2,1)} reshape(bf16[128,16,2,16]{3,2,1,0:T(2,128)(2,1)S(1)} %copy.64) | data formatting | bytes 262144
  104.8 6.3 %all-to-all-start.1 = ((bf16[64,2,512]{2,1,0:T(2,128)(2,1)}), bf16[64,2,512]{2,1,0:T(2,128)(2,1)S(1)}, u32[]{:S(2)}, u32[]{:S(2)}) async-start(bf16[64,2,512]{2,1,0:T(2,128)(2,1)} %reshape.139), calls=%async_computation.1 | async-start | bytes 262144 | tf_op jit(solution)/shard_map/all_to_all | solution.py:58
  111.3 10.9 %all-to-all-done.1 = bf16[64,2,512]{2,1,0:T(2,128)(2,1)S(1)} async-done(((bf16[64,2,512]{2,1,0:T(2,128)(2,1)}), bf16[64,2,512]{2,1,0:T(2,128)(2,1)S(1)}, u32[]{:S(2)}, u32[]{:S(2)}) %all-to-all-start.1) | async-done | bytes 131104 | tf_op jit(solution)/shard_map/all_to_all | solution.py:58
  122.2 0.7 reshape.140
  122.9 0.2 copy.65
  123.1 0.7 copy.66
  123.8 1.1 reshape.132
  124.9 6.7 %convolution_bitcast_fusion = f32[2,16,2,2,2,64]{5,4,3,2,1,0:T(2,128)S(1)} fusion(bf16[2,16,2,2,64,512]{5,4,3,2,1,0:T(8,128)(2,1)} %param.6, bf16[2,16,2,2,512,1]{4,3,2,1,0,5:T(2,128)(2,1)S(1)} %bitcast.74), kind=kOutput, calls=%fused_computation | convolution fusion | flops 16777216 | bytes 8585216 | tf_op jit(solution)/shard_map/scprkb,scqpb->scprqk/dot_general | solution.py:62
  131.8 0.1 copy.70
  131.9 0.2 reshape.141
  132.1 8.0 %all_to_all.51 = bf16[4,2,1024]{2,1,0:T(2,128)(2,1)S(1)} all-to-all(bf16[4,2,1024]{2,1,0:T(2,128)(2,1)S(1)} %reshape.141), channel_id=1, replica_groups=mesh['tm'=64,'freq'=4] {'freq'}, dimensions={0} | all-to-all | bytes 32768 | tf_op jit(solution)/shard_map/all_to_all | solution.py:73
  140.1 0.1 reshape.142
  140.5 0.2 convolution_bitcast_fusion.1
  140.8 0.6 copy.74
  (19 shorter events, 0.7 us)
Async XLA Ops:
  0.0 140.5 %copy-start = (bf16[2,2,64,64]{3,2,1,0:T(8,128)(2,1)S(1)}, bf16[2,2,64,64]{3,2,1,0:T(8,128)(2,1)}, u32[]{:S(2)}) copy-start(bf16[2,2,64,64]{3,2,1,0:T(8,128)(2,1)} %param.7) | copy-start | bytes 98308
  0.0 38.3 %copy-start.2 = (s32[128]{0:T(128)S(1)}, s32[128]{0:T(128)}, u32[]{:S(2)}) copy-start(s32[128]{0:T(128)} %param.8) | copy-start | bytes 1540
  25.2 41.3 %all-to-all-start = ((bf16[64,2,4096]{2,1,0:T(2,128)(2,1)}), bf16[64,2,4096]{2,1,0:T(2,128)(2,1)S(1)}, u32[]{:S(2)}, u32[]{:S(2)}) async-start(bf16[64,2,4096]{2,1,0:T(2,128)(2,1)} %reshape.137), calls=%async_computation | async-start | bytes 2097152 | tf_op jit(solution)/shard_map/all_to_all | solution.py:56
  86.1 25.0 %copy-start.1 = (s32[2,16,2]{1,2,0:T(2,128)S(1)}, s32[2,16,2]{1,2,0:T(2,128)}, u32[]{:S(2)}) copy-start(s32[2,16,2]{1,2,0:T(2,128)} %param.9) | copy-start | bytes 772
  104.8 17.4 %all-to-all-start.1 = ((bf16[64,2,512]{2,1,0:T(2,128)(2,1)}), bf16[64,2,512]{2,1,0:T(2,128)(2,1)S(1)}, u32[]{:S(2)}, u32[]{:S(2)}) async-start(bf16[64,2,512]{2,1,0:T(2,128)(2,1)} %reshape.139), calls=%async_computation.1 | async-start | bytes 262144 | tf_op jit(solution)/shard_map/all_to_all | solution.py:58
where the time goes:
time: 142 us; the launch traced here: 141 us
  local copies, waits for them, and re-layouts  66.7 us (47%)
  waiting for transfers between devices  36.5 us (26%)
  starting transfers between devices  19.4 us (14%)
  blocking collectives  8.02 us (6%)
  matrix products  7.64 us (5%)
  other arithmetic  2.89 us (2%)
    unnamed x14, local copies, waits for them, and re-layouts  35.6 us
    all_to_all x2, local copies, waits for them, and re-layouts, shards(): lax.all_to_all(visibilities, 'tm', split_axis=3, concat_axis=2, tiled=True)  27.2 us
    all_to_all x1, waiting for transfers between devices, shards(): lax.all_to_all(visibilities, 'tm', split_axis=3, concat_axis=2, tiled=True)  25.7 us
    all_to_all x1, starting transfers between devices, shards(): lax.all_to_all(visibilities, 'tm', split_axis=3, concat_axis=2, tiled=True)  13.2 us
    all_to_all x1, waiting for transfers between devices, shards(): lax.all_to_all(local_modes, 'tm', split_axis=0, concat_axis=3, tiled=True)  10.9 us
    all_to_all x1, blocking collectives, shards(): lax.all_to_all(projected, 'freq', split_axis=4, concat_axis=1, tiled=True)  8.02 us
    dot_general x1, matrix products, shards(): jnp.einsum('scprkb,scqpb->scprqk', projection, mode_spectra, preferred_el...  6.71 us
    all_to_all x1, starting transfers between devices, shards(): lax.all_to_all(local_modes, 'tm', split_axis=0, concat_axis=3, tiled=True)  6.28 us
  transfers between devices with their start and end apart: 2, of which 2 were waited for; matrix products, arithmetic and copies ran while one was open for 2% of the time, Pallas kernels for 0%

commit v1 on v0

v1 whole, which is shorter than its diff:
```python
import functools
import math

import jax
import jax.numpy as jnp
from jax import lax
from jax.experimental import pallas as pl
from jax.experimental.pallas import tpu as pltpu
from jax.sharding import PartitionSpec as P

MESH = pl.DeviceIdType.MESH
F32 = jnp.float32
BF16 = jnp.bfloat16

ZN = 8
GN = 8
XN = 4
NC = 4
CC = 4
SENDS = ((1, 0), (3, 0), (2, 0), (0, 1), (1, 1), (3, 1), (2, 1))


def iota(shape, dim):
    return lax.broadcasted_iota(jnp.int32, shape, dim)


def cosine_of(phase):
    angle = (jnp.abs(phase - 512) - 256).astype(F32) * (2.0 * math.pi / 1024)
    square = angle * angle
    series = F32(1.0 / math.factorial(13))
    for order in (11, 9, 7, 5, 3, 1):
        sign = 1.0 if (order // 2) % 2 == 0 else -1.0
        series = series * square + F32(sign / math.factorial(order))
    return series * angle


def kernel(
    vis, proj, kl, az, live, out,
    vis_v, streams, proj_v, table, partial, b_send, b_recv, final, c_send, c_recv, d_recv, klw, mixed,
    load_sem, self_sem, proj_sem, a_ssem, a_rsem, b_ssem, b_rsem, c_ssem, c_rsem, d_ssem, d_rsem,
):
    tm = lax.axis_index("tm")
    x = lax.axis_index("freq")
    z = tm // GN
    g = lax.rem(tm, GN)
    y = g // 2
    core = lax.rem(g, 2)

    def in_plane(dy, dc):
        return lax.rem(y + dy, 4) * 2 + lax.rem(core + dc, 2)

    def plane_device(peer):
        return (z * GN + peer, x)

    def z_device(dz):
        return (lax.rem(z + dz + ZN, ZN) * GN + g, x)

    def x_peer(dx):
        return lax.rem(x + dx, XN)

    peers = [in_plane(dy, dc) for dy, dc in SENDS]
    others = [plane_device(peer) for peer in peers]
    others += [z_device(1), z_device(-1)]
    others += [(tm, x_peer(dx)) for dx in (1, 2, 3)]

    barrier = pltpu.get_barrier_semaphore()
    for device in others:
        pl.semaphore_signal(barrier, inc=1, device_id=device, device_id_type=MESH)

    def load(slot, block):
        columns = pl.ds(pl.multiple_of(block * 128, 128), 128)
        return pltpu.make_async_copy(vis.at[:, :, :, columns], vis_v.at[slot], load_sem.at[slot])

    my_rows = pl.ds(pl.multiple_of(g * 16, 16), 16)
    my_columns = pl.ds(pl.multiple_of(g * 128, 128), 128)
    own = pltpu.make_async_copy(vis.at[:, :, :, my_columns], streams.at[:, :, my_rows, :], self_sem)
    loads = [load(slot, peer) for slot, peer in enumerate(peers)]
    for copy in loads:
        copy.start()
    own.start()
    proj_loads = [
        pltpu.make_async_copy(
            proj.at[:, n * CC : (n + 1) * CC], proj_v.at[:, n * CC : (n + 1) * CC], proj_sem.at[n]
        )
        for n in range(NC)
    ]
    pl.semaphore_wait(barrier, len(others))

    pending = []

    def a_copy(n, slot, peer):
        channels = pl.ds(n * CC, CC)
        return pltpu.make_async_remote_copy(
            src_ref=vis_v.at[slot, :, channels],
            dst_ref=streams.at[:, channels, my_rows, :],
            send_sem=a_ssem.at[n, slot],
            recv_sem=a_rsem.at[n, slot],
            device_id=plane_device(peer),
            device_id_type=MESH,
        )

    a_copies = [[a_copy(n, slot, peer) for slot, peer in enumerate(peers)] for n in range(NC)]
    for n in range(NC):
        for slot in range(len(peers)):
            if n == 0:
                loads[slot].wait()
            a_copies[n][slot].start()
            pending.append(a_copies[n][slot])
    for copy in proj_loads:
        copy.start()

    row = iota((256, 128), 0)
    lane = iota((256, 128), 1)
    slot_of_row = (row >> 5) * 16 + (row & 7) * 2 + ((row >> 4) & 1)
    order = jnp.sum(jnp.where(lane == slot_of_row, az[...], 0.0), axis=1, keepdims=True)
    row = iota((256, 256), 0)
    lane = iota((256, 256), 1)
    time = z * 128 + (lane & 127)
    quarter = (row >> 3) & 1
    phase = order.astype(jnp.int32) * time + 256 * quarter - 256 * (lane >> 7)
    values = cosine_of(phase & 1023) * F32(1.0 / 32.0)
    upper = values.astype(BF16)
    table[:, :256] = upper
    table[:, 256:] = (values - upper.astype(F32)).astype(BF16)

    chan = iota((64, 256), 0)
    col = iota((64, 256), 1)
    col_chan = (col >> 6) * 16 + ((col >> 4) & 3) * 4 + ((col >> 1) & 3)
    for s in range(2):
        hit = (chan == col_chan) & (((col >> 3) & 1) == s)
        even = jnp.where(hit & ((col & 1) == 0), 1.0, 0.0).astype(BF16)
        odd = jnp.where(hit & ((col & 1) == 1), 1.0, 0.0).astype(BF16)
        w_re, w_im = kl[s, 0], kl[s, 1]
        dot = functools.partial(jnp.dot, preferred_element_type=F32)
        klw[s * 128 : s * 128 + 64] = (dot(w_re, even) - dot(w_im, odd)).astype(BF16)
        klw[s * 128 + 64 : s * 128 + 128] = (dot(w_im, even) + dot(w_re, odd)).astype(BF16)

    def chain(n, forward):
        return 4 if (n % 2 == 0) == forward else 3

    def b_copy(n, way, i):
        return pltpu.make_async_remote_copy(
            src_ref=b_send.at[n, way, i],
            dst_ref=b_recv.at[n, way, i],
            send_sem=b_ssem.at[n, way, i],
            recv_sem=b_rsem.at[n, way, i],
            device_id=z_device(1 if way == 0 else -1),
            device_id_type=MESH,
        )

    def own_part(n, dz):
        plane = lax.rem(z + dz + 2 * ZN, ZN)
        return partial[n, pl.ds(pl.multiple_of(plane * 32, 32), 32), :]

    def dft(n):
        if n == 0:
            own.wait()
        for copy in a_copies[n]:
            copy.wait_recv()
        blocks = []
        for c in range(n * CC, (n + 1) * CC):
            both = jnp.concatenate([streams[0, c], streams[1, c]], axis=0)
            blocks.append(jnp.concatenate([both, both], axis=0))
        samples = jnp.concatenate(blocks, axis=1)
        partial[n] = jnp.dot(table[...], samples, preferred_element_type=F32)
        for way in range(2):
            length = chain(n, way == 0)
            b_send[n, way, 0] = own_part(n, length if way == 0 else -length).astype(BF16)
            copy = b_copy(n, way, 0)
            copy.start()
            pending.append(copy)

    def forward(n, i):
        for way in range(2):
            length = chain(n, way == 0)
            if i < length:
                b_copy(n, way, i - 1).wait_recv()
                left = length - i
                term = own_part(n, left if way == 0 else -left)
                b_send[n, way, i] = (b_recv[n, way, i - 1].astype(F32) + term).astype(BF16)
                copy = b_copy(n, way, i)
                copy.start()
                pending.append(copy)

    def c_copy(n, slot, peer):
        return pltpu.make_async_remote_copy(
            src_ref=c_send.at[n, peer],
            dst_ref=c_recv.at[n, g],
            send_sem=c_ssem.at[n, slot],
            recv_sem=c_rsem.at[n, slot],
            device_id=plane_device(peer),
            device_id_type=MESH,
        )

    def finish(n):
        total = own_part(n, 0)
        for way in range(2):
            last = chain(n, way == 0) - 1
            b_copy(n, way, last).wait_recv()
            total = total + b_recv[n, way, last].astype(F32)
        for s in range(2):
            for c in range(CC):
                for q in range(2):
                    at = ((s * CC + c) * 2 + q) * 8
                    rows = (s * 2 + q) * 8
                    final[n, at : at + 8, :] = total[rows : rows + 8, c * 128 : (c + 1) * 128]
        for peer in range(GN):
            c_send[n, peer] = final[n, pl.ds(peer, 16, stride=8), :].astype(BF16)
        for slot, peer in enumerate(peers):
            copy = c_copy(n, slot, peer)
            copy.start()
            pending.append(copy)
        c_recv[n, g] = c_send[n, g]

    def d_copy(n, dx):
        return pltpu.make_async_remote_copy(
            src_ref=d_recv.at[x, n],
            dst_ref=d_recv.at[x, n],
            send_sem=d_ssem.at[n, dx - 1],
            recv_sem=d_rsem.at[n, dx - 1],
            device_id=(tm, x_peer(dx)),
            device_id_type=MESH,
        )

    def project(n):
        proj_loads[n].wait()
        for slot, peer in enumerate(peers):
            c_copy(n, slot, peer).wait_recv()
        row = iota((16, 128), 0)
        lane = iota((16, 128), 1)
        wide_row = iota((16, 512), 0)
        raw = []
        live_count = []
        for p in range(2):
            vectors = jnp.concatenate([c_recv[n, 4 * p + j] for j in range(4)], axis=1)
            total = jnp.zeros((16, 128), F32)
            count = jnp.zeros((16, 128), jnp.int32)
            for s in range(2):
                for c in range(CC):
                    slot = s * CC + c
                    picked = jnp.where((wide_row >> 1) == slot, vectors, jnp.zeros_like(vectors))
                    matrix = proj_v[s, n * CC + c, p].reshape(128, 512)
                    total = total + lax.dot_general(
                        picked, matrix, (((1,), (1,)), ((), ())), preferred_element_type=F32
                    )
                    count = jnp.where((row >> 1) == slot, live[s, p, n * CC + c], count)
            raw.append(total)
            live_count.append(count)

        def swap_parts(v):
            return jnp.where((row & 1) == 0, pltpu.roll(v, 15, 0), pltpu.roll(v, 1, 0))

        sign = jnp.where((row & 1) == 0, -1.0, 1.0)
        low = raw[0] + sign * swap_parts(pltpu.roll(raw[0], 64, 1))
        high = pltpu.roll(raw[1], 64, 1) + sign * swap_parts(raw[1])
        modes = jnp.where(lane < 64, low, high)
        count = jnp.where(lane < 64, live_count[0], live_count[1])
        d_recv[x, n] = jnp.where((lane & 63) < count, modes, 0.0).astype(BF16)
        for dx in (1, 2, 3):
            copy = d_copy(n, dx)
            copy.start()
            pending.append(copy)

    for step in range(NC + 5):
        if step < NC:
            dft(step)
        for i in (1, 2, 3):
            if 0 <= step - i < NC:
                forward(step - i, i)
        if 0 <= step - 4 < NC:
            finish(step - 4)
        if 0 <= step - 5 < NC:
            project(step - 5)

    for n in range(NC):
        for dx in (1, 2, 3):
            d_copy(n, dx).wait_recv()
    gathered = d_recv[...].reshape(256, 128)
    for s in range(2):
        block = jnp.dot(klw[s * 128 : (s + 1) * 128], gathered, preferred_element_type=F32)
        mixed[s] = jnp.transpose(block)
        for p in range(2):
            rows = mixed[s, pl.ds(pl.multiple_of(p * 64 + x * 16, 16), 16), :]
            for q in range(2):
                out[s, q, p] = rows[:, q * 64 : (q + 1) * 64]
    for copy in pending:
        copy.wait_send()


def shards(visibilities, projection, kl_weight, azimuthal, live_mode_totals):
    hbm = pl.BlockSpec(memory_space=pl.ANY)
    vmem = pl.BlockSpec(memory_space=pltpu.VMEM)
    smem = pl.BlockSpec(memory_space=pltpu.SMEM)
    dma = pltpu.SemaphoreType.DMA
    out = pl.pallas_call(
        kernel,
        out_shape=jax.ShapeDtypeStruct((2, 2, 2, 16, 64), F32),
        in_specs=[hbm, hbm, vmem, vmem, smem],
        out_specs=vmem,
        scratch_shapes=[
            pltpu.VMEM((7, 2, 16, 16, 128), BF16),
            pltpu.VMEM((2, 16, 128, 128), BF16),
            pltpu.VMEM((2, 16, 2, 2, 64, 512), BF16),
            pltpu.VMEM((256, 512), BF16),
            pltpu.VMEM((NC, 256, 512), F32),
            pltpu.VMEM((NC, 2, 4, 32, 512), BF16),
            pltpu.VMEM((NC, 2, 4, 32, 512), BF16),
            pltpu.VMEM((NC, 128, 128), F32),
            pltpu.VMEM((NC, GN, 16, 128), BF16),
            pltpu.VMEM((NC, GN, 16, 128), BF16),
            pltpu.VMEM((XN, NC, 16, 128), BF16),
            pltpu.VMEM((256, 256), BF16),
            pltpu.VMEM((2, 128, 128), F32),
            dma((7,)),
            dma,
            dma((NC,)),
            dma((NC, 7)),
            dma((NC, 7)),
            dma((NC, 2, 4)),
            dma((NC, 2, 4)),
            dma((NC, 7)),
            dma((NC, 7)),
            dma((NC, 3)),
            dma((NC, 3)),
        ],
        compiler_params=pltpu.CompilerParams(
            collective_id=0, has_side_effects=True, vmem_limit_bytes=48 * 1024 * 1024
        ),
        name="mmode",
    )(
        visibilities,
        projection,
        kl_weight,
        azimuthal.astype(F32).reshape(1, 128),
        jnp.transpose(live_mode_totals, (0, 2, 1)),
    )
    return jnp.transpose(out, (0, 1, 4, 2, 3))


def solution(mesh):
    return jax.shard_map(
        shards,
        mesh=mesh,
        in_specs=(
            P(None, "freq", "tm", None),
            P("tm", "freq", None, None, None, None),
            P("tm", None, None, None),
            P(),
            P("tm", "freq", None),
        ),
        out_specs=P("tm", None, None, None, "freq"),
        check_vma=False,
    )
```

time: 142 us -> 50.1 us (0.35)
  local copies, waits for them, and re-layouts: 66.7 us -> 3.38 us
  Pallas kernels: 0 us -> 45.8 us
  waiting for transfers between devices: 36.5 us -> 0 us
  starting transfers between devices: 19.4 us -> 0 us
  blocking collectives: 8.02 us -> 0 us
  matrix products: 7.64 us -> 0 us
  other arithmetic: 2.89 us -> 0.66 us
    pallas_call x0 -> x1, Pallas kernels: none -> 45.8 us  [shards(): pl.pallas_call(kernel, out_shape=jax.ShapeDtypeStruct((2, 2, 2, 16, 64),...]
    all_to_all x2 -> x0, waiting for transfers between devices: 36.5 us -> none  [the longest x1 25.7 us: shards(): lax.all_to_all(visibilities, 'tm', split_axis=3, concat_axis=2, tiled=True)]
    unnamed x14 -> x7, local copies, waits for them, and re-layouts: 35.6 us -> 3.38 us
    all_to_all x6 -> x0, local copies, waits for them, and re-layouts: 28.3 us -> none  [the longest x2 27.2 us: shards(): lax.all_to_all(visibilities, 'tm', split_axis=3, concat_axis=2, tiled=True)]
    all_to_all x2 -> x0, starting transfers between devices: 19.4 us -> none  [the longest x1 13.2 us: shards(): lax.all_to_all(visibilities, 'tm', split_axis=3, concat_axis=2, tiled=True)]
    all_to_all x1 -> x0, blocking collectives: 8.02 us -> none  [shards(): lax.all_to_all(projected, 'freq', split_axis=4, concat_axis=1, tiled=True)]
    dot_general x3 -> x0, matrix products: 7.64 us -> none  [the longest x1 6.71 us: shards(): jnp.einsum('scprkb,scqpb->scprqk', projection, mode_spectra, preferred_el...]
    convert_element_type x3 -> x0, other arithmetic: 2.56 us -> none  [the longest x1 2.48 us: split_table(): upper = table.astype(jnp.bfloat16)]
  transfers between devices with their start and end apart: 2 -> 0, of which waited for: 2 -> 0; matrix products, arithmetic and copies ran while one was open for 2% -> 0% of each run, Pallas kernels for 0% -> 0%
where the time goes in v1:
time: 50.1 us; the launch traced here: 49.9 us
  Pallas kernels  45.8 us (91%)
  local copies, waits for them, and re-layouts  3.38 us (7%)
  other arithmetic  0.66 us (1%)
    pallas_call x1, Pallas kernels, shards(): pl.pallas_call(kernel, out_shape=jax.ShapeDtypeStruct((2, 2, 2, 16, 64),...  45.8 us
    unnamed x7, local copies, waits for them, and re-layouts  3.38 us

profile of v1, /device:TPU:1, one launch (start us, length us, event | category | flops | bytes accessed | tf_op | source)
XLA Modules:
  0.0 49.9 jit_solution(3975947155397333706)
XLA Ops:
  0.0 0.7 %convert_bitcast_fusion.az = f32[1,128]{1,0:T(1,128)S(1)} fusion(s32[128]{0:T(128)} %param.8), kind=kLoop, calls=%fused_computation | loop fusion | flops 128 | bytes 1024 | tf_op jit(solution)/shard_map/reshape | solution.py:334
  0.7 0.0 copy-start
  0.7 1.2 %copy-done = bf16[2,16,16,1024]{3,2,1,0:T(8,128)(2,1)S(1)} copy-done((bf16[2,16,16,1024]{3,2,1,0:T(8,128)(2,1)S(1)}, bf16[2,16,16,1024]{3,2,1,0:T(8,128)(2,1)}, u32[]{:S(2)}) %copy-start) | copy-done | bytes 1048600
  1.9 0.0 copy-start.1
  1.9 0.8 %copy-done.1 = bf16[2,2,64,64]{3,2,1,0:T(8,128)(2,1)S(1)} copy-done((bf16[2,2,64,64]{3,2,1,0:T(8,128)(2,1)S(1)}, bf16[2,2,64,64]{3,2,1,0:T(8,128)(2,1)}, u32[]{:S(2)}) %copy-start.1) | copy-done | bytes 32792
  2.7 0.0 copy-start.2
  2.7 0.7 %copy-done.2 = s32[2,16,2]{1,2,0:T(2,128)S(1)} copy-done((s32[2,16,2]{1,2,0:T(2,128)S(1)}, s32[2,16,2]{1,2,0:T(2,128)}, u32[]{:S(2)}) %copy-start.2) | copy-done | bytes 280
  3.4 45.8 %mmode.1 = f32[2,2,2,16,64]{4,3,2,1,0:T(8,128)S(1)} custom-call(bf16[2,16,16,1024]{3,2,1,0:T(8,128)(2,1)S(1)} %copy-done, bf16[2,16,2,2,64,512]{5,4,3,2,1,0:T(8,128)(2,1)} %proj.1, bf16[2,2,64,64]{3,2,1,0:T(8,128)(2,1)S(1)} %copy-done.1, f32[1,128]{1,0:T(1,128)S(1)} %convert_bitcast_fusion.az, s32[2,2,16]{2,1,0:T(2,128)S(1)} %bitcast.5), custom_call_target="tpu_custom_call" | custom-call | tf_op jit(solution)/shard_map/mmode/pallas_call | solution.py:295
  49.2 0.6 %copy.7 = f32[2,2,64,2,16]{2,4,3,1,0:T(8,128)} copy(f32[2,2,64,2,16]{2,4,3,1,0:T(8,128)S(1)} %bitcast.4) | data formatting | bytes 65536
Async XLA Ops:
  0.7 1.2 %copy-start = (bf16[2,16,16,1024]{3,2,1,0:T(8,128)(2,1)S(1)}, bf16[2,16,16,1024]{3,2,1,0:T(8,128)(2,1)}, u32[]{:S(2)}) copy-start(bf16[2,16,16,1024]{3,2,1,0:T(8,128)(2,1)} %vis.1) | copy-start | bytes 3145732
  1.9 0.8 %copy-start.1 = (bf16[2,2,64,64]{3,2,1,0:T(8,128)(2,1)S(1)}, bf16[2,2,64,64]{3,2,1,0:T(8,128)(2,1)}, u32[]{:S(2)}) copy-start(bf16[2,2,64,64]{3,2,1,0:T(8,128)(2,1)} %kl.1) | copy-start | bytes 98308
  2.7 0.7 %copy-start.2 = (s32[2,16,2]{1,2,0:T(2,128)S(1)}, s32[2,16,2]{1,2,0:T(2,128)}, u32[]{:S(2)}) copy-start(s32[2,16,2]{1,2,0:T(2,128)} %param.9) | copy-start | bytes 772

commit v2 on v1

v2 whole, which is shorter than its diff:
```python
import functools
import math

import jax
import jax.numpy as jnp
from jax import lax
from jax.experimental import pallas as pl
from jax.experimental.pallas import tpu as pltpu
from jax.sharding import PartitionSpec as P

MESH = pl.DeviceIdType.MESH
F32 = jnp.float32
BF16 = jnp.bfloat16

ZN = 8
GN = 8
XN = 4
NC = 4
CC = 4
NH = 8
HC = 2
WAYS = ((0, 1), (1, -1))
CHAINS = 3
FIRST, NEXT, HOP, FAR, CROSS = 7.0, 1.35, 3.0, 3.6, 3.4
SENDS = ((1, 0), (3, 0), (2, 0), (0, 1), (1, 1), (3, 1), (2, 1))


def iota(shape, dim):
    return lax.broadcasted_iota(jnp.int32, shape, dim)


def cosine_of(phase):
    angle = (jnp.abs(phase - 512) - 256).astype(F32) * (2.0 * math.pi / 1024)
    square = angle * angle
    series = F32(1.0 / math.factorial(13))
    for order in (11, 9, 7, 5, 3, 1):
        sign = 1.0 if (order // 2) % 2 == 0 else -1.0
        series = series * square + F32(sign / math.factorial(order))
    return series * angle


def kernel(
    vis, proj, kl_hbm, az_hbm, live_hbm, out,
    kl, az, live, vis_v, streams, proj_v, table, partial, b_send, b_recv, final, c_send, c_recv, d_recv, klw, mixed,
    small_sem, load_sem, self_sem, proj_sem, a_ssem, a_rsem, b_ssem, b_rsem, c_ssem, c_rsem, d_ssem, d_rsem,
):
    tm = lax.axis_index("tm")
    x = lax.axis_index("freq")
    z = tm // GN
    g = lax.rem(tm, GN)
    y = g // 2
    core = lax.rem(g, 2)

    def in_plane(dy, dc):
        return lax.rem(y + dy, 4) * 2 + lax.rem(core + dc, 2)

    def plane_device(peer):
        return (z * GN + peer, x)

    def z_device(dz):
        return (lax.rem(z + dz + ZN, ZN) * GN + g, x)

    def x_peer(dx):
        return lax.rem(x + dx, XN)

    peers = [in_plane(dy, dc) for dy, dc in SENDS]
    others = [plane_device(peer) for peer in peers]
    others += [z_device(1), z_device(-1), z_device(2), z_device(-2)]
    others += [(tm, x_peer(dx)) for dx in (1, 2, 3)]

    barrier = pltpu.get_barrier_semaphore()
    for device in others:
        pl.semaphore_signal(barrier, inc=1, device_id=device, device_id_type=MESH)

    def load(slot, block):
        columns = pl.ds(pl.multiple_of(block * 128, 128), 128)
        return pltpu.make_async_copy(vis.at[:, :, :, columns], vis_v.at[slot], load_sem.at[slot])

    my_rows = pl.ds(pl.multiple_of(g * 16, 16), 16)
    my_columns = pl.ds(pl.multiple_of(g * 128, 128), 128)
    own = pltpu.make_async_copy(vis.at[:, :, :, my_columns], streams.at[:, :, my_rows, :], self_sem)
    loads = [load(slot, peer) for slot, peer in enumerate(peers)]
    smalls = [
        pltpu.make_async_copy(source, target, small_sem.at[k])
        for k, (source, target) in enumerate(((az_hbm, az), (kl_hbm, kl), (live_hbm, live)))
    ]
    for copy in loads:
        copy.start()
    own.start()
    for copy in smalls:
        copy.start()
    proj_loads = [
        pltpu.make_async_copy(
            proj.at[:, n * CC : (n + 1) * CC], proj_v.at[:, n * CC : (n + 1) * CC], proj_sem.at[n]
        )
        for n in range(NC)
    ]
    with jax.named_scope("enter"):
        pl.semaphore_wait(barrier, len(others))

    def wait_bytes(sem, ref):
        pltpu.make_async_copy(ref, ref, sem).wait()

    def a_copy(n, slot, peer):
        channels = pl.ds(n * HC, HC)
        return pltpu.make_async_remote_copy(
            src_ref=vis_v.at[slot, :, channels],
            dst_ref=streams.at[:, channels, my_rows, :],
            send_sem=a_ssem,
            recv_sem=a_rsem.at[n],
            device_id=plane_device(peer),
            device_id_type=MESH,
        )

    a_copies = [[a_copy(n, slot, peer) for slot, peer in enumerate(peers)] for n in range(NH)]
    with jax.named_scope("send"):
        for n in range(NH):
            for slot in range(len(peers)):
                if n == 0:
                    loads[slot].wait()
                a_copies[n][slot].start()
        for copy in proj_loads:
            copy.start()

    for copy in smalls:
        copy.wait()
    row = iota((256, 128), 0)
    lane = iota((256, 128), 1)
    slot_of_row = (row >> 5) * 16 + (row & 7) * 2 + ((row >> 4) & 1)
    order = jnp.sum(jnp.where(lane == slot_of_row, az[...].astype(F32), 0.0), axis=1, keepdims=True)
    row = iota((256, 256), 0)
    lane = iota((256, 256), 1)
    time = z * 128 + (lane & 127)
    quarter = (row >> 3) & 1
    phase = order.astype(jnp.int32) * time + 256 * quarter - 256 * (lane >> 7)
    values = cosine_of(phase & 1023) * F32(1.0 / 32.0)
    upper = values.astype(BF16)
    table[:, :256] = upper
    table[:, 256:] = (values - upper.astype(F32)).astype(BF16)

    chan = iota((64, 256), 0)
    col = iota((64, 256), 1)
    col_chan = (col >> 6) * 16 + ((col >> 4) & 3) * 4 + ((col >> 1) & 3)
    for s in range(2):
        hit = (chan == col_chan) & (((col >> 3) & 1) == s)
        even = jnp.where(hit & ((col & 1) == 0), 1.0, 0.0).astype(BF16)
        odd = jnp.where(hit & ((col & 1) == 1), 1.0, 0.0).astype(BF16)
        w_re, w_im = kl[s, 0], kl[s, 1]
        dot = functools.partial(jnp.dot, preferred_element_type=F32)
        klw[s * 128 : s * 128 + 64] = (dot(w_re, even) - dot(w_im, odd)).astype(BF16)
        klw[s * 128 + 64 : s * 128 + 128] = (dot(w_im, even) + dot(w_re, odd)).astype(BF16)

    def chain(n, forward):
        return 4 if (n % 2 == 0) == forward else 3

    def b_start(n, slot, dz, value, group):
        b_send[n, slot] = value.astype(BF16)
        pltpu.make_async_remote_copy(
            src_ref=b_send.at[n, slot],
            dst_ref=b_recv.at[n, slot],
            send_sem=b_ssem,
            recv_sem=b_rsem.at[n, group],
            device_id=z_device(dz),
            device_id_type=MESH,
        ).start()

    def b_take(n, group, slots):
        wait_bytes(b_rsem.at[n, group], b_send.at[n, pl.ds(0, len(slots))])
        return [b_recv[n, slot].astype(F32) for slot in slots]

    def own_part(n, dz):
        plane = lax.rem(z + dz + 2 * ZN, ZN)
        return partial[n, pl.ds(pl.multiple_of(plane * 32, 32), 32), :]

    def dft(n):
        if n == 0:
            own.wait()
        wait_bytes(a_rsem.at[n], vis_v.at[:, :, pl.ds(n * HC, HC)])
        blocks = []
        for c in range(n * HC, (n + 1) * HC):
            both = jnp.concatenate([streams[0, c], streams[1, c]], axis=0)
            blocks.append(jnp.concatenate([both, both], axis=0))
        samples = jnp.concatenate(blocks, axis=1)
        partial[n] = jnp.dot(table[...], samples, preferred_element_type=F32)
        if n < CHAINS:
            for way, dz in WAYS:
                b_start(n, 4 * way, dz, own_part(n, dz * chain(n, way == 0)), 0)
        else:
            far = 2 if n % 2 == 0 else -2
            b_start(n, 2, far, own_part(n, 2 * far), 0)
            b_start(n, 0, 1, own_part(n, 3), 0)
            b_start(n, 1, -1, own_part(n, -3), 0)
            b_start(n, 3, 1, own_part(n, 1), 1)
            b_start(n, 4, -1, own_part(n, -1), 1)

    def forward(n, i):
        ways = [(way, dz) for way, dz in WAYS if chain(n, way == 0) > i]
        came = b_take(n, i - 1, [4 * way + i - 1 for way, _ in ways])
        for (way, dz), value in zip(ways, came, strict=True):
            left = chain(n, way == 0) - i
            b_start(n, 4 * way + i, dz, value + own_part(n, dz * left), 3 if left == 1 else i)

    def relay(n):
        came = b_take(n, 0, [0, 1, 2])
        came[n % 2] = came[n % 2] + came[2]
        for way, dz in WAYS:
            b_start(n, 5 + way, 2 * dz, came[way] + own_part(n, 2 * dz), 1)

    def last_slots(n):
        if n < CHAINS:
            return 3, [4 * way + chain(n, way == 0) - 1 for way, _ in WAYS]
        return 1, [3, 4, 5, 6]

    def c_copy(n, peer):
        return pltpu.make_async_remote_copy(
            src_ref=c_send.at[n, peer],
            dst_ref=c_recv.at[n, g],
            send_sem=c_ssem,
            recv_sem=c_rsem.at[n],
            device_id=plane_device(peer),
            device_id_type=MESH,
        )

    def finish(n):
        for half in range(2):
            h = 2 * n + half
            total = own_part(h, 0)
            for value in b_take(h, *last_slots(h)):
                total = total + value
            for s in range(2):
                for c in range(HC):
                    for q in range(2):
                        at = ((s * CC + half * HC + c) * 2 + q) * 8
                        rows = (s * 2 + q) * 8
                        final[n, at : at + 8, :] = total[rows : rows + 8, c * 128 : (c + 1) * 128]
        for peer in range(GN):
            c_send[n, peer] = final[n, pl.ds(peer, 16, stride=8), :].astype(BF16)
        for peer in peers:
            c_copy(n, peer).start()
        c_recv[n, g] = c_send[n, g]

    def d_copy(n, dx):
        return pltpu.make_async_remote_copy(
            src_ref=d_recv.at[x, n],
            dst_ref=d_recv.at[x, n],
            send_sem=d_ssem,
            recv_sem=d_rsem,
            device_id=(tm, x_peer(dx)),
            device_id_type=MESH,
        )

    def project(n):
        proj_loads[n].wait()
        wait_bytes(c_rsem.at[n], c_send.at[n, pl.ds(0, 7)])
        row = iota((16, 128), 0)
        lane = iota((16, 128), 1)
        wide_row = iota((16, 512), 0)
        raw = []
        live_count = []
        for p in range(2):
            vectors = jnp.concatenate([c_recv[n, 4 * p + j] for j in range(4)], axis=1)
            total = jnp.zeros((16, 128), F32)
            count = jnp.zeros((16, 128), jnp.int32)
            for s in range(2):
                for c in range(CC):
                    slot = s * CC + c
                    picked = jnp.where((wide_row >> 1) == slot, vectors, jnp.zeros_like(vectors))
                    matrix = proj_v[s, n * CC + c, p].reshape(128, 512)
                    total = total + lax.dot_general(
                        picked, matrix, (((1,), (1,)), ((), ())), preferred_element_type=F32
                    )
                    count = jnp.where((row >> 1) == slot, live[s, p, n * CC + c], count)
            raw.append(total)
            live_count.append(count)

        def swap_parts(v):
            return jnp.where((row & 1) == 0, pltpu.roll(v, 15, 0), pltpu.roll(v, 1, 0))

        sign = jnp.where((row & 1) == 0, -1.0, 1.0)
        low = raw[0] + sign * swap_parts(pltpu.roll(raw[0], 64, 1))
        high = pltpu.roll(raw[1], 64, 1) + sign * swap_parts(raw[1])
        modes = jnp.where(lane < 64, low, high)
        count = jnp.where(lane < 64, live_count[0], live_count[1])
        d_recv[x, n] = jnp.where((lane & 63) < count, modes, 0.0).astype(BF16)
        for dx in (1, 2, 3):
            d_copy(n, dx).start()

    tasks = []
    ready = []
    for h in range(NH):
        begin = FIRST + NEXT * h
        tasks.append((begin, f"dft{h}", functools.partial(dft, h)))
        if h < CHAINS:
            for i in (1, 2, 3):
                tasks.append((begin + HOP * i, f"fwd{h}_{i}", functools.partial(forward, h, i)))
            ready.append(begin + HOP * 4)
        else:
            tasks.append((begin + HOP, f"rel{h}", functools.partial(relay, h)))
            ready.append(begin + HOP + FAR)
    for n in range(NC):
        begin = max(ready[2 * n : 2 * n + 2])
        tasks.append((begin, f"fin{n}", functools.partial(finish, n)))
        tasks.append((begin + CROSS, f"prj{n}", functools.partial(project, n)))
    for _, name, task in sorted(tasks, key=lambda entry: entry[0]):
        with jax.named_scope(name):
            task()

    with jax.named_scope("dwait"):
        wait_bytes(d_rsem, d_recv.at[pl.ds(0, 3)])
    with jax.named_scope("mix"):
        gathered = d_recv[...].reshape(256, 128)
        for s in range(2):
            block = jnp.dot(klw[s * 128 : (s + 1) * 128], gathered, preferred_element_type=F32)
            mixed[s] = jnp.transpose(block)
            for p in range(2):
                rows = mixed[s, pl.ds(pl.multiple_of(p * 64 + x * 16, 16), 16), :]
                for q in range(2):
                    out[s, q, p] = rows[:, q * 64 : (q + 1) * 64]
    with jax.named_scope("drain"):
        wait_bytes(a_ssem, vis_v)
        wait_bytes(b_ssem, b_send.at[:, pl.ds(0, 7)])
        wait_bytes(c_ssem, c_send.at[:, pl.ds(0, 7)])
        wait_bytes(d_ssem, d_recv.at[pl.ds(0, 3)])


def shards(visibilities, projection, kl_weight, azimuthal, live_mode_totals):
    hbm = pl.BlockSpec(memory_space=pltpu.HBM)
    vmem = pl.BlockSpec(memory_space=pltpu.VMEM)
    dma = pltpu.SemaphoreType.DMA
    out = pl.pallas_call(
        kernel,
        out_shape=jax.ShapeDtypeStruct((2, 2, 2, 16, 64), F32),
        in_specs=[hbm] * 5,
        out_specs=vmem,
        scratch_shapes=[
            pltpu.VMEM((2, 2, 64, 64), BF16),
            pltpu.VMEM((1, 128), jnp.int32),
            pltpu.SMEM((2, 2, 16), jnp.int32),
            pltpu.VMEM((7, 2, 16, 16, 128), BF16),
            pltpu.VMEM((2, 16, 128, 128), BF16),
            pltpu.VMEM((2, 16, 2, 2, 64, 512), BF16),
            pltpu.VMEM((256, 512), BF16),
            pltpu.VMEM((NH, 256, 256), F32),
            pltpu.VMEM((NH, 8, 32, 256), BF16),
            pltpu.VMEM((NH, 8, 32, 256), BF16),
            pltpu.VMEM((NC, 128, 128), F32),
            pltpu.VMEM((NC, GN, 16, 128), BF16),
            pltpu.VMEM((NC, GN, 16, 128), BF16),
            pltpu.VMEM((XN, NC, 16, 128), BF16),
            pltpu.VMEM((256, 256), BF16),
            pltpu.VMEM((2, 128, 128), F32),
            dma((3,)),
            dma((7,)),
            dma,
            dma((NC,)),
            dma,
            dma((NH,)),
            dma,
            dma((NH, 4)),
            dma,
            dma((NC,)),
            dma,
            dma,
        ],
        compiler_params=pltpu.CompilerParams(
            collective_id=0, has_side_effects=True, vmem_limit_bytes=67043328
        ),
        name="mmode",
    )(
        visibilities,
        projection,
        kl_weight,
        azimuthal.reshape(1, 128),
        jnp.transpose(live_mode_totals, (0, 2, 1)),
    )
    return jnp.transpose(out, (0, 1, 4, 2, 3))


def solution(mesh):
    return jax.shard_map(
        shards,
        mesh=mesh,
        in_specs=(
            P(None, "freq", "tm", None),
            P("tm", "freq", None, None, None, None),
            P("tm", None, None, None),
            P(),
            P("tm", "freq", None),
        ),
        out_specs=P("tm", None, None, None, "freq"),
        check_vma=False,
    )
```

time: 50.1 us -> 43.1 us (0.86)
  Pallas kernels: 45.8 us -> 41.5 us
  local copies, waits for them, and re-layouts: 3.38 us -> 1.47 us
  other arithmetic: 0.66 us -> 0 us
    pallas_call x1, Pallas kernels: 45.8 us -> 41.5 us  [shards(): pl.pallas_call(kernel, out_shape=jax.ShapeDtypeStruct((2, 2, 2, 16, 64),...]
    unnamed x7 -> x1, local copies, waits for them, and re-layouts: 3.38 us -> 1.47 us
    reshape x1 -> x0, other arithmetic: 0.66 us -> none  [shards(): azimuthal.astype(F32).reshape(1, 128)]
where the time goes in v2:
time: 43.1 us; the launch traced here: 43 us
  Pallas kernels  41.5 us (96%)
  local copies, waits for them, and re-layouts  1.47 us (3%)
    pallas_call x1, Pallas kernels, shards(): pl.pallas_call(kernel, out_shape=jax.ShapeDtypeStruct((2, 2, 2, 16, 64),...  41.5 us
    unnamed x1, local copies, waits for them, and re-layouts  1.47 us

profile of v2, /device:TPU:1, one launch (start us, length us, event | category | flops | bytes accessed | tf_op | source)
XLA Modules:
  0.0 43.0 jit_solution(16593354169563855764)
XLA Ops:
  0.0 41.5 %mmode.1 = f32[2,2,2,16,64]{4,3,2,1,0:T(8,128)} custom-call(bf16[2,16,16,1024]{3,2,1,0:T(8,128)(2,1)} %vis.1, bf16[2,16,2,2,64,512]{5,4,3,2,1,0:T(8,128)(2,1)} %proj.1, bf16[2,2,64,64]{3,2,1,0:T(8,128)(2,1)} %kl_hbm.1, s32[1,128]{1,0:T(1,128)} %bitcast.5, s32[2,2,16]{2,1,0:T(2,128)} %bitcast.4), custom_call_target="tpu_custom_call" | custom-call | tf_op jit(solution)/shard_map/mmode/pallas_call | solution.py:330
  41.5 1.5 %copy.7 = f32[2,2,64,2,16]{2,4,3,1,0:T(8,128)} copy(f32[2,2,64,2,16]{2,4,3,1,0:T(8,128)} %bitcast.3) | data formatting | bytes 65536

commit v3 on v2

--- a/solution.py
+++ b/solution.py
@@ -20,9 +20,10 @@
 NH = 8
 HC = 2
 WAYS = ((0, 1), (1, -1))
-CHAINS = 3
-FIRST, NEXT, HOP, FAR, CROSS = 7.0, 1.35, 3.0, 3.6, 3.4
+CHAIN, TRIPLE, PAIRS = 3, 2, 1
+KINDS = (TRIPLE, TRIPLE, TRIPLE, TRIPLE, PAIRS, PAIRS, PAIRS, PAIRS)
 SENDS = ((1, 0), (3, 0), (2, 0), (0, 1), (1, 1), (3, 1), (2, 1))
+ORDER = ('dft0', 'dft1', 'dft2', 'dft3', 'fwd0_1', 'dft4', 'fwd1_1', 'dft5', 'fwd2_1', 'dft6', 'fwd3_1', 'fwd0_2', 'dft7', 'fwd4_1', 'fwd1_2', 'fwd5_1', 'fwd2_2', 'fwd6_1', 'fwd3_2', 'fwd7_1', 'fin0', 'fin2', 'fin1', 'fin3', 'prj0', 'prj2', 'prj1', 'prj3')
 
 
 def iota(shape, dim):
@@ -182,7 +183,7 @@
             blocks.append(jnp.concatenate([both, both], axis=0))
         samples = jnp.concatenate(blocks, axis=1)
         partial[n] = jnp.dot(table[...], samples, preferred_element_type=F32)
-        if n < CHAINS:
+        if KINDS[n] == CHAIN:
             for way, dz in WAYS:
                 b_start(n, 4 * way, dz, own_part(n, dz * chain(n, way == 0)), 0)
         else:
@@ -190,26 +191,31 @@
             b_start(n, 2, far, own_part(n, 2 * far), 0)
             b_start(n, 0, 1, own_part(n, 3), 0)
             b_start(n, 1, -1, own_part(n, -3), 0)
-            b_start(n, 3, 1, own_part(n, 1), 1)
-            b_start(n, 4, -1, own_part(n, -1), 1)
+            if KINDS[n] == PAIRS:
+                b_start(n, 3, 1, own_part(n, 1), 3)
+                b_start(n, 4, -1, own_part(n, -1), 3)
 
     def forward(n, i):
-        ways = [(way, dz) for way, dz in WAYS if chain(n, way == 0) > i]
-        came = b_take(n, i - 1, [4 * way + i - 1 for way, _ in ways])
-        for (way, dz), value in zip(ways, came, strict=True):
-            left = chain(n, way == 0) - i
-            b_start(n, 4 * way + i, dz, value + own_part(n, dz * left), 3 if left == 1 else i)
-
-    def relay(n):
-        came = b_take(n, 0, [0, 1, 2])
-        came[n % 2] = came[n % 2] + came[2]
-        for way, dz in WAYS:
-            b_start(n, 5 + way, 2 * dz, came[way] + own_part(n, 2 * dz), 1)
+        if KINDS[n] == CHAIN:
+            ways = [(way, dz) for way, dz in WAYS if chain(n, way == 0) > i]
+            came = b_take(n, i - 1, [4 * way + i - 1 for way, _ in ways])
+            for (way, dz), value in zip(ways, came, strict=True):
+                left = chain(n, way == 0) - i
+                b_start(n, 4 * way + i, dz, value + own_part(n, dz * left), 3 if left == 1 else i)
+        elif i == 1:
+            came = b_take(n, 0, [0, 1, 2])
+            came[n % 2] = came[n % 2] + came[2]
+            for way, dz in WAYS:
+                step, group = (2 * dz, 3) if KINDS[n] == PAIRS else (dz, 1)
+                b_start(n, 5 + way, step, came[way] + own_part(n, 2 * dz), group)
+        else:
+            for (way, dz), value in zip(WAYS, b_take(n, 1, [5, 6]), strict=True):
+                b_start(n, 3 + way, dz, value + own_part(n, dz), 3)
 
     def last_slots(n):
-        if n < CHAINS:
+        if KINDS[n] == CHAIN:
             return 3, [4 * way + chain(n, way == 0) - 1 for way, _ in WAYS]
-        return 1, [3, 4, 5, 6]
+        return 3, [3, 4, 5, 6] if KINDS[n] == PAIRS else [3, 4]
 
     def c_copy(n, peer):
         return pltpu.make_async_remote_copy(
@@ -254,7 +260,6 @@
         wait_bytes(c_rsem.at[n], c_send.at[n, pl.ds(0, 7)])
         row = iota((16, 128), 0)
         lane = iota((16, 128), 1)
-        wide_row = iota((16, 512), 0)
         raw = []
         live_count = []
         for p in range(2):
@@ -262,14 +267,14 @@
             total = jnp.zeros((16, 128), F32)
             count = jnp.zeros((16, 128), jnp.int32)
             for s in range(2):
+                matrix = proj_v[s, n * CC : (n + 1) * CC, p].reshape(CC * 128, 512)
+                products = lax.dot_general(
+                    vectors, matrix, (((1,), (1,)), ((), ())), preferred_element_type=F32
+                )
                 for c in range(CC):
-                    slot = s * CC + c
-                    picked = jnp.where((wide_row >> 1) == slot, vectors, jnp.zeros_like(vectors))
-                    matrix = proj_v[s, n * CC + c, p].reshape(128, 512)
-                    total = total + lax.dot_general(
-                        picked, matrix, (((1,), (1,)), ((), ())), preferred_element_type=F32
-                    )
-                    count = jnp.where((row >> 1) == slot, live[s, p, n * CC + c], count)
+                    mine = (row >> 1) == s * CC + c
+                    total = jnp.where(mine, products[:, c * 128 : (c + 1) * 128], total)
+                    count = jnp.where(mine, live[s, p, n * CC + c], count)
             raw.append(total)
             live_count.append(count)
 
@@ -285,25 +290,18 @@
         for dx in (1, 2, 3):
             d_copy(n, dx).start()
 
-    tasks = []
-    ready = []
+    tasks = {}
     for h in range(NH):
-        begin = FIRST + NEXT * h
-        tasks.append((begin, f"dft{h}", functools.partial(dft, h)))
-        if h < CHAINS:
-            for i in (1, 2, 3):
-                tasks.append((begin + HOP * i, f"fwd{h}_{i}", functools.partial(forward, h, i)))
-            ready.append(begin + HOP * 4)
-        else:
-            tasks.append((begin + HOP, f"rel{h}", functools.partial(relay, h)))
-            ready.append(begin + HOP + FAR)
+        tasks[f"dft{h}"] = functools.partial(dft, h)
+        for i in range(1, KINDS[h] + 1):
+            tasks[f"fwd{h}_{i}"] = functools.partial(forward, h, i)
     for n in range(NC):
-        begin = max(ready[2 * n : 2 * n + 2])
-        tasks.append((begin, f"fin{n}", functools.partial(finish, n)))
-        tasks.append((begin + CROSS, f"prj{n}", functools.partial(project, n)))
-    for _, name, task in sorted(tasks, key=lambda entry: entry[0]):
+        tasks[f"fin{n}"] = functools.partial(finish, n)
+        tasks[f"prj{n}"] = functools.partial(project, n)
+    assert sorted(tasks) == sorted(ORDER)
+    for name in ORDER:
         with jax.named_scope(name):
-            task()
+            tasks[name]()
 
     with jax.named_scope("dwait"):
         wait_bytes(d_rsem, d_recv.at[pl.ds(0, 3)])
@@ -327,6 +325,7 @@
     hbm = pl.BlockSpec(memory_space=pltpu.HBM)
     vmem = pl.BlockSpec(memory_space=pltpu.VMEM)
     dma = pltpu.SemaphoreType.DMA
+    keep = functools.partial(pltpu.with_memory_space_constraint, memory_space=pltpu.HBM)
     out = pl.pallas_call(
         kernel,
         out_shape=jax.ShapeDtypeStruct((2, 2, 2, 16, 64), F32),
@@ -363,15 +362,15 @@
             dma,
         ],
         compiler_params=pltpu.CompilerParams(
-            collective_id=0, has_side_effects=True, vmem_limit_bytes=67043328
+            collective_id=0, has_side_effects=True, vmem_limit_bytes=48 * 1024 * 1024
         ),
         name="mmode",
     )(
-        visibilities,
-        projection,
-        kl_weight,
-        azimuthal.reshape(1, 128),
-        jnp.transpose(live_mode_totals, (0, 2, 1)),
+        keep(visibilities),
+        keep(projection),
+        keep(kl_weight),
+        keep(azimuthal.reshape(1, 128)),
+        keep(jnp.transpose(live_mode_totals, (0, 2, 1))),
     )
     return jnp.transpose(out, (0, 1, 4, 2, 3))
 

time: 43.1 us -> 40.6 us (0.942)
  Pallas kernels: 41.5 us -> 39.9 us
  local copies, waits for them, and re-layouts: 1.47 us -> 0.63 us
    pallas_call x1, Pallas kernels: 41.5 us -> 39.9 us  [shards(): pl.pallas_call(kernel, out_shape=jax.ShapeDtypeStruct((2, 2, 2, 16, 64),...]
    unnamed x1, local copies, waits for them, and re-layouts: 1.47 us -> 0.63 us
where the time goes in v3:
time: 40.6 us; the launch traced here: 40.5 us
  Pallas kernels  39.9 us (98%)
  local copies, waits for them, and re-layouts  0.63 us (2%)
    pallas_call x1, Pallas kernels, shards(): pl.pallas_call(kernel, out_shape=jax.ShapeDtypeStruct((2, 2, 2, 16, 64),...  39.9 us

profile of v3, /device:TPU:1, one launch (start us, length us, event | category | flops | bytes accessed | tf_op | source)
XLA Modules:
  0.0 40.5 jit_solution(2193162783379417965)
XLA Ops:
  0.0 39.9 %mmode.1 = f32[2,2,2,16,64]{4,3,2,1,0:T(8,128)S(1)} custom-call(bf16[2,16,16,1024]{3,2,1,0:T(8,128)(2,1)} %vis.1, bf16[2,16,2,2,64,512]{5,4,3,2,1,0:T(8,128)(2,1)} %proj.1, bf16[2,2,64,64]{3,2,1,0:T(8,128)(2,1)} %kl_hbm.1, s32[1,128]{1,0:T(1,128)} %bitcast.5, s32[2,2,16]{2,1,0:T(2,128)} %bitcast.4), custom_call_target="tpu_custom_call" | custom-call | tf_op jit(solution)/shard_map/mmode/pallas_call | solution.py:329
  39.9 0.6 %copy.7 = f32[2,2,64,2,16]{2,4,3,1,0:T(8,128)} copy(f32[2,2,64,2,16]{2,4,3,1,0:T(8,128)S(1)} %bitcast.3) | data formatting | bytes 65536

commit v4 on v3

--- a/solution.py
+++ b/solution.py
@@ -21,9 +21,9 @@
 HC = 2
 WAYS = ((0, 1), (1, -1))
 CHAIN, TRIPLE, PAIRS = 3, 2, 1
-KINDS = (TRIPLE, TRIPLE, TRIPLE, TRIPLE, PAIRS, PAIRS, PAIRS, PAIRS)
+KINDS = (PAIRS, PAIRS, TRIPLE, TRIPLE, TRIPLE, TRIPLE, PAIRS, PAIRS)
 SENDS = ((1, 0), (3, 0), (2, 0), (0, 1), (1, 1), (3, 1), (2, 1))
-ORDER = ('dft0', 'dft1', 'dft2', 'dft3', 'fwd0_1', 'dft4', 'fwd1_1', 'dft5', 'fwd2_1', 'dft6', 'fwd3_1', 'fwd0_2', 'dft7', 'fwd4_1', 'fwd1_2', 'fwd5_1', 'fwd2_2', 'fwd6_1', 'fwd3_2', 'fwd7_1', 'fin0', 'fin2', 'fin1', 'fin3', 'prj0', 'prj2', 'prj1', 'prj3')
+ORDER = ('pre0', 'pre1', 'pre2', 'dft0', 'pre3', 'dft1', 'dft2', 'dft3', 'fwd0_1', 'dft4', 'fwd1_1', 'dft5', 'fwd2_1', 'dft6', 'fwd3_1', 'dft7', 'fwd4_1', 'fin0', 'fwd2_2', 'fwd5_1', 'fwd6_1', 'fwd3_2', 'fwd7_1', 'fwd4_2', 'prj0', 'fwd5_2', 'fin1', 'fin3', 'fin2', 'prj1', 'prj3', 'prj2')
 
 
 def iota(shape, dim):
@@ -42,7 +42,7 @@
 
 def kernel(
     vis, proj, kl_hbm, az_hbm, live_hbm, out,
-    kl, az, live, vis_v, streams, proj_v, table, partial, b_send, b_recv, final, c_send, c_recv, d_recv, klw, mixed,
+    kl, az, live, vis_v, streams, proj_v, proj_t, table, partial, b_send, b_recv, final, c_send, c_recv, d_recv, klw, mixed,
     small_sem, load_sem, self_sem, proj_sem, a_ssem, a_rsem, b_ssem, b_rsem, c_ssem, c_rsem, d_ssem, d_rsem,
 ):
     tm = lax.axis_index("tm")
@@ -255,8 +255,14 @@
             device_id_type=MESH,
         )
 
+    def prepare(n):
+        proj_loads[n].wait()
+        for s in range(2):
+            for p in range(2):
+                matrix = proj_v[s, n * CC : (n + 1) * CC, p].reshape(CC * 128, 512)
+                proj_t[n, s, p] = jnp.transpose(matrix)
+
     def project(n):
-        proj_loads[n].wait()
         wait_bytes(c_rsem.at[n], c_send.at[n, pl.ds(0, 7)])
         row = iota((16, 128), 0)
         lane = iota((16, 128), 1)
@@ -267,10 +273,7 @@
             total = jnp.zeros((16, 128), F32)
             count = jnp.zeros((16, 128), jnp.int32)
             for s in range(2):
-                matrix = proj_v[s, n * CC : (n + 1) * CC, p].reshape(CC * 128, 512)
-                products = lax.dot_general(
-                    vectors, matrix, (((1,), (1,)), ((), ())), preferred_element_type=F32
-                )
+                products = jnp.dot(vectors, proj_t[n, s, p], preferred_element_type=F32)
                 for c in range(CC):
                     mine = (row >> 1) == s * CC + c
                     total = jnp.where(mine, products[:, c * 128 : (c + 1) * 128], total)
@@ -298,6 +301,7 @@
     for n in range(NC):
         tasks[f"fin{n}"] = functools.partial(finish, n)
         tasks[f"prj{n}"] = functools.partial(project, n)
+        tasks[f"pre{n}"] = functools.partial(prepare, n)
     assert sorted(tasks) == sorted(ORDER)
     for name in ORDER:
         with jax.named_scope(name):
@@ -338,6 +342,7 @@
             pltpu.VMEM((7, 2, 16, 16, 128), BF16),
             pltpu.VMEM((2, 16, 128, 128), BF16),
             pltpu.VMEM((2, 16, 2, 2, 64, 512), BF16),
+            pltpu.VMEM((NC, 2, 2, 512, 512), BF16),
             pltpu.VMEM((256, 512), BF16),
             pltpu.VMEM((NH, 256, 256), F32),
             pltpu.VMEM((NH, 8, 32, 256), BF16),

time: 40.6 us -> 40.1 us (0.988)
  Pallas kernels: 39.9 us -> 39.4 us
    pallas_call x1, Pallas kernels: 39.9 us -> 39.4 us  [shards(): pl.pallas_call(kernel, out_shape=jax.ShapeDtypeStruct((2, 2, 2, 16, 64),...]
where the time goes in v4:
time: 40.1 us; the launch traced here: 40 us
  Pallas kernels  39.4 us (98%)
  local copies, waits for them, and re-layouts  0.63 us (2%)
    pallas_call x1, Pallas kernels, shards(): pl.pallas_call(kernel, out_shape=jax.ShapeDtypeStruct((2, 2, 2, 16, 64),...  39.4 us

profile of v4, /device:TPU:1, one launch (start us, length us, event | category | flops | bytes accessed | tf_op | source)
XLA Modules:
  0.0 40.0 jit_solution(16559719668163371614)
XLA Ops:
  0.0 39.4 %mmode.1 = f32[2,2,2,16,64]{4,3,2,1,0:T(8,128)S(1)} custom-call(bf16[2,16,16,1024]{3,2,1,0:T(8,128)(2,1)} %vis.1, bf16[2,16,2,2,64,512]{5,4,3,2,1,0:T(8,128)(2,1)} %proj.1, bf16[2,2,64,64]{3,2,1,0:T(8,128)(2,1)} %kl_hbm.1, s32[1,128]{1,0:T(1,128)} %bitcast.5, s32[2,2,16]{2,1,0:T(2,128)} %bitcast.4), custom_call_target="tpu_custom_call" | custom-call | tf_op jit(solution)/shard_map/mmode/pallas_call | solution.py:333
  39.4 0.6 %copy.7 = f32[2,2,64,2,16]{2,4,3,1,0:T(8,128)} copy(f32[2,2,64,2,16]{2,4,3,1,0:T(8,128)S(1)} %bitcast.3) | data formatting | bytes 65536
